TPU v7x, 128 devices: a whole 4x4x4 slice. The times are simulated.
128 devices in a mesh: row: 8 (over z, core), col: 16 (over y, x).
Axes of the slice: x: 4, y: 4, z: 4, core: 2. Of those that a mesh axis runs over, the one named last changes fastest.
Arguments:
- ainv_anc: bfloat16 [24576, 24576], P('row', 'col'), may hold values from -6 to 6
- l_panel: bfloat16 [1536, 24576], P('col', 'row'), may hold values from -0.078125 to 0.078125
- diag_inv: float32 [1536, 768], P('col', 'row'), may hold values from -6 to 6
- struct_mask: int32 [2, 192], replicated, may hold values 0 or 1
- pieces: float32 [24576, 32, 128], P(('row', 'col')), may hold values from -6 to 6
- tile_owner: int32 [24576, 1], P(('row', 'col')), may hold values from 0 to 127; in each aligned block of 192 rows (0 to 191, 192 to 383, ...) at most 3 rows name the same one
Outputs:
- ainv_upper: bfloat16 [1536, 24576], P('col', 'row')
- ainv_diag: float32 [1536, 768], P('col', 'row')
- moved: float32 [49152, 32, 128], P(('row', 'col'))
Inputs may be any that keep to these rules, and one draw needn't show every extreme that they name: `tile_owner`: among the 192 pieces of one device no owner is named more than 3 times, a bound that some block reaches.
All inputs are finite; a program needn't handle non-finite values.
Results may differ from a plain program's by a relative error of at most 0.015.
Values may be sent and summed in bfloat16 or wider, within the bound.
A program may use at most 128 MiB of HBM per device.

v0:
```python
import jax
import jax.numpy as jnp
from jax import lax
from jax.sharding import PartitionSpec as P

W = 768
AB = 128
SLOT = 3


def broadcast(value, axis, root):
    mine = lax.axis_index(axis) == root
    return lax.psum(jnp.where(mine, value, jnp.zeros_like(value)), axis)


def cut_along(value, dim, count):
    before, after = (value.shape[:dim], value.shape[dim + 1 :])
    return jnp.moveaxis(value.reshape(*before, count, -1, *after), dim, 0)


def sum_at_owner(value, axis, dim):
    parts = cut_along(value, dim, lax.axis_size(axis))
    arrived = lax.all_to_all(parts, axis, split_axis=0, concat_axis=0, tiled=True)
    return arrived.astype(jnp.float32).sum(axis=0)


def joined_along(parts, dim):
    shape = list(parts.shape[1:])
    shape[dim] *= parts.shape[0]
    return jnp.moveaxis(parts, 0, dim).reshape(shape)


def joined_exchange(value, axis, axes, splits, concats):
    sizes = [lax.axis_size(a) for a in axes]
    parts = cut_along(value, splits[0], sizes[0])
    parts = jnp.moveaxis(cut_along(parts, splits[1] + 1, sizes[1]), 0, 1)
    inside = parts.shape[2:]
    parts = parts.reshape(-1, *inside)
    parts = lax.all_to_all(parts, axis, split_axis=0, concat_axis=0, tiled=True)
    parts = joined_along(parts.reshape(*sizes, *inside), concats[0] + 1)
    return joined_along(parts, concats[1])


def local(ainv_anc, l_panel, diag_inv, struct_mask, pieces, tile_owner):
    row_devices = lax.axis_size("row")
    col_devices = lax.axis_size("col")
    row_index = lax.axis_index("row")
    col_index = lax.axis_index("col")
    slab_rows = l_panel.shape[0]
    local_rows = l_panel.shape[1]
    cross_width = ainv_anc.shape[1]
    group_ratio = col_devices // row_devices
    supernode = col_index * slab_rows // W
    block_count = local_rows // AB
    keep_blocks = lax.dynamic_slice(
        struct_mask, (supernode, row_index * block_count), (1, block_count)
    )
    keep_rows = (
        jnp.broadcast_to(keep_blocks[:, :, None], (1, block_count, AB)).reshape(1, local_rows) > 0
    )
    masked = jnp.where(keep_rows, l_panel, jnp.zeros_like(l_panel))
    gathered = lax.all_gather(masked, "col", axis=0, tiled=True)
    offset = col_index % group_ratio * cross_width
    own_cross = lax.dynamic_slice_in_dim(gathered, offset, cross_width, 1)
    cross_rows = broadcast(own_cross, "row", col_index // group_ratio)
    product = lax.psum_scatter(
        lax.dot_general(
            cross_rows, ainv_anc, (((1,), (1,)), ((), ())), preferred_element_type=jnp.float32
        ).astype(jnp.bfloat16),
        "col",
        scatter_dimension=0,
        tiled=True,
    ).astype(jnp.float32)
    upper_rows = jnp.where(keep_rows, -product, jnp.zeros_like(product)).astype(jnp.bfloat16)
    own_block = lax.dynamic_slice_in_dim(gathered, supernode * W, W, 0)
    diag_part = lax.dot_general(
        upper_rows, own_block, (((1,), (1,)), ((), ())), preferred_element_type=jnp.float32
    )
    summed = sum_at_owner(diag_part.astype(jnp.bfloat16), "row", 1)
    ainv_diag = diag_inv - summed
    devices_all = row_devices * col_devices
    owners = tile_owner[:, 0]
    onehot = (owners[:, None] == jnp.arange(devices_all, dtype=jnp.int32)[None, :]).astype(
        jnp.int32
    )
    earlier = jnp.cumsum(onehot, axis=0) - onehot
    rank_in_dest = jnp.sum(earlier * onehot, axis=1)
    slot_index = owners * SLOT + rank_in_dest
    piece_rows = pieces.shape[1]
    piece_cols = pieces.shape[2]
    buffer = (
        jnp.zeros((devices_all * SLOT, piece_rows, piece_cols), jnp.float32)
        .at[slot_index]
        .set(pieces)
    )
    shaped = buffer.reshape(row_devices, col_devices, SLOT, piece_rows, piece_cols)
    arrived = joined_exchange(
        shaped.astype(jnp.bfloat16), ("row", "col"), ("row", "col"), (0, 1), (0, 1)
    ).astype(shaped.dtype)
    moved_pieces = arrived.reshape(devices_all * SLOT, piece_rows, piece_cols)
    return (upper_rows, ainv_diag, moved_pieces)


def solution(mesh):
    in_specs = (
        P("row", "col"),
        P("col", "row"),
        P("col", "row"),
        P(),
        P(("row", "col"), None, None),
        P(("row", "col"), None),
    )
    out_specs = (P("col", "row"), P("col", "row"), P(("row", "col"), None, None))
    return jax.shard_map(local, mesh=mesh, in_specs=in_specs, out_specs=out_specs, check_vma=False)
```

profile of v0, /device:TPU:1, one launch (start us, length us, event | category | flops | bytes accessed | tf_op | source)
XLA Modules:
  0.0 332.0 jit_solution(8603867656916050667)
XLA Ops:
  7.2 0.8 compare_bitcast_fusion
  8.1 1.9 broadcast_select_fusion
  10.1 79.1 %all-gather.2.cloned.1.call-done = bf16[1536,3072]{1,0:T(8,128)(2,1)} async-done(((bf16[96,3072]{1,0:T(8,128)(2,1)}), bf16[1536,3072]{1,0:T(8,128)(2,1)}) %all-gather.2.cloned.1.call-update) | async-done | bytes 9437200 | tf_op jit(solution)/shard_map/all_gather | solution.py:62
  89.2 5.3 %dynamic-slice_select_fusion = bf16[1536,1536]{1,0:T(8,128)(2,1)} fusion(bf16[1536,3072]{1,0:T(8,128)(2,1)} %all-gather.2.cloned.1.call-done, s32[]{:T(128)S(6)} %select_n.53, pred[]{:T(512)S(6)} %eq.27), kind=kLoop, calls=%fused_computation.4 | loop fusion | flops 2359296 | bytes 9437189 | tf_op jit(solution)/shard_map/jit(_where)/select_n | solution.py:13
  94.6 72.9 %all-reduce.3.cloned.1.call-done = bf16[1536,1536]{1,0:T(8,128)(2,1)} async-done(((bf16[1536,1536]{1,0:T(8,128)(2,1)}), bf16[1536,1536]{1,0:T(8,128)(2,1)}) %all-reduce.3.cloned.1.call-update) | async-done | bytes 4718608 | tf_op jit(solution)/shard_map/psum | solution.py:13
  167.5 20.3 %convolution_convert_fusion = bf16[1536,3072]{1,0:T(8,128)(2,1)} fusion(bf16[1536,1536]{1,0:T(8,128)(2,1)} %all-reduce.3.cloned.1.call-done, bf16[3072,1536]{1,0:T(8,128)(2,1)} %param.6), kind=kOutput, calls=%fused_computation.1 | convolution fusion | flops 14500233216 | bytes 23592960 | tf_op jit(solution)/shard_map/dot_general | solution.py:67
  187.8 0.6 copy-done.3
  188.5 0.1 iota_compare_fusion
  188.6 0.1 fusion.5
  188.8 0.2 fusion.8
  189.0 3.5 %broadcast_in_dim.39 = f32[384,32,128]{2,1,0:T(8,128)} broadcast(f32[]{:T(128)} %constant.65.clone.1), dimensions={} | broadcast | bytes 6291460 | tf_op jit(solution)/shard_map/broadcast_in_dim | solution.py:92
  192.5 23.5 %scatter_fusion = f32[384,32,128]{2,1,0:T(8,128)} fusion(f32[384,32,128]{2,1,0:T(8,128)} %broadcast_in_dim.39, s32[192]{0:T(256)S(1)} %bitcast.46, f32[192,32,128]{2,1,0:T(8,128)S(1)} %copy-done), kind=kCustom, calls=%fused_computation | custom fusion | bytes 9437952 | tf_op jit(solution)/shard_map/scatter | solution.py:94
  216.0 5.3 %convert_element_type.54 = bf16[384,32,128]{2,1,0:T(8,128)(2,1)} convert(f32[384,32,128]{2,1,0:T(8,128)} %scatter_fusion) | non-fusion elementwise | flops 1572864 | bytes 9437184 | tf_op jit(solution)/shard_map/convert_element_type | solution.py:98
  221.3 9.8 %all-to-all-start.1 = ((bf16[128,1,1,3,32,128]{5,4,3,2,1,0:T(8,128)(2,1)}), bf16[128,1,1,3,32,128]{5,4,3,2,1,0:T(8,128)(2,1)S(1)}, u32[]{:S(2)}, u32[]{:S(2)}) async-start(bf16[128,1,1,3,32,128]{5,4,3,2,1,0:T(8,128)(2,1)} %bitcast.38), calls=%async_computation.2 | async-start | bytes 6291456 | tf_op jit(solution)/shard_map/all_to_all | solution.py:39
  231.2 74.3 %reduce-scatter.2.cloned.1.call-done = bf16[96,3072]{1,0:T(8,128)(2,1)} async-done(((bf16[1536,3072]{1,0:T(8,128)(2,1)}), bf16[96,3072]{1,0:T(8,128)(2,1)}) %reduce-scatter.2.cloned.1.call-update) | async-done | bytes 589840 | tf_op jit(solution)/shard_map/reduce_scatter | solution.py:66
  305.5 1.2 select_convert_fusion
  306.7 0.8 copy-done.1
  307.5 3.9 %fusion.2 = bf16[96,768]{1,0:T(8,128)(2,1)S(1)} fusion(bf16[96,3072]{1,0:T(8,128)(2,1)S(1)} %select_convert_fusion, bf16[1536,3072]{1,0:T(8,128)(2,1)} %all-gather.2.cloned.1.call-done, s32[]{:T(128)S(6)} %select_n.56), kind=kOutput, calls=%fused_computation.7 | convolution fusion | flops 453058560 | bytes 5455876 | tf_op jit(solution)/shard_map/dot_general | solution.py:76
  311.5 0.2 reshape.62
  311.7 0.7 copy.18
  312.4 6.5 %all-to-all-start = ((bf16[8,96,96]{2,1,0:T(8,128)(2,1)}), bf16[8,96,96]{2,1,0:T(8,128)(2,1)S(1)}, u32[]{:S(2)}, u32[]{:S(2)}) async-start(bf16[8,96,96]{2,1,0:T(8,128)(2,1)} %bitcast.34), calls=%async_computation.1 | async-start | bytes 393216 | tf_op jit(solution)/shard_map/all_to_all | solution.py:23
  318.9 3.8 %bitcast_convert_fusion = f32[384,32,128]{2,1,0:T(8,128)} fusion(bf16[128,1,1,3,32,128]{5,4,3,2,1,0:T(8,128)(2,1)S(1)} %all-to-all-done.1), kind=kLoop, calls=%fused_computation.5 | loop fusion | flops 1572864 | bytes 9437184 | tf_op jit(solution)/shard_map/convert_element_type | solution.py:99
  322.7 2.1 all-to-all-done
  324.8 0.6 sub.15
  (23 shorter events, 0.4 us)
Async XLA Ops:
  7.2 82.0 %all-gather.2.cloned.1.call-start = ((), (), s32[]{:S(2)}) async-start(), calls=%async_computation.3 | async-start | bytes 10027008 | tf_op jit(solution)/shard_map/all_gather | solution.py:62
  10.0 157.4 %all-reduce.3.cloned.1.call-start = ((), (), s32[]{:S(2)}) async-start(), calls=%async_computation.4 | async-start | bytes 9437184 | tf_op jit(solution)/shard_map/psum | solution.py:13
  94.5 211.0 %reduce-scatter.2.cloned.1.call-start = ((), (), s32[]{:S(2)}) async-start(), calls=%async_computation.5 | async-start | bytes 10027008 | tf_op jit(solution)/shard_map/reduce_scatter | solution.py:66
  187.8 0.7 copy-start.3
  187.8 4.7 %copy-start = (f32[192,32,128]{2,1,0:T(8,128)S(1)}, f32[192,32,128]{2,1,0:T(8,128)}, u32[]{:S(2)}) copy-start(f32[192,32,128]{2,1,0:T(8,128)} %param.10) | copy-start | bytes 9437188
  221.3 91.1 %all-to-all-start.1 = ((bf16[128,1,1,3,32,128]{5,4,3,2,1,0:T(8,128)(2,1)}), bf16[128,1,1,3,32,128]{5,4,3,2,1,0:T(8,128)(2,1)S(1)}, u32[]{:S(2)}, u32[]{:S(2)}) async-start(bf16[128,1,1,3,32,128]{5,4,3,2,1,0:T(8,128)(2,1)} %bitcast.38), calls=%async_computation.2 | async-start | bytes 6291456 | tf_op jit(solution)/shard_map/all_to_all | solution.py:39
  306.7 0.8 copy-start.1
  312.4 12.3 %all-to-all-start = ((bf16[8,96,96]{2,1,0:T(8,128)(2,1)}), bf16[8,96,96]{2,1,0:T(8,128)(2,1)S(1)}, u32[]{:S(2)}, u32[]{:S(2)}) async-start(bf16[8,96,96]{2,1,0:T(8,128)(2,1)} %bitcast.34), calls=%async_computation.1 | async-start | bytes 393216 | tf_op jit(solution)/shard_map/all_to_all | solution.py:23
  318.9 5.9 %copy-start.2 = (f32[96,96]{1,0:T(8,128)S(1)}, f32[96,96]{1,0:T(8,128)}, u32[]{:S(2)}) copy-start(f32[96,96]{1,0:T(8,128)} %param.8) | copy-start | bytes 110596
Sparse Core Ops, SparseCore 0:
  10.7 78.4 all-gather.1
  94.6 72.7 all-reduce.2
  187.9 117.5 reduce-scatter.1
where the time goes:
time: 333 us; the launch traced here: 332 us
  waiting for transfers between devices  228 us (68%)
  local copies, waits for them, and re-layouts  29.5 us (9%)
  matrix products  24.3 us (7%)
  other arithmetic  19.5 us (6%)
  starting transfers between devices  16.4 us (5%)
  between operations  13.9 us (4%)
    all_gather x1, waiting for transfers between devices, local(): gathered = lax.all_gather(masked, 'col', axis=0, tiled=True)  79.1 us
    reduce_scatter x1, waiting for transfers between devices, local(): lax.psum_scatter(lax.dot_general(cross_rows, ainv_anc, (((1,), (1,)), (()...  74.3 us
    psum x1, waiting for transfers between devices, broadcast(): return lax.psum(jnp.where(mine, value, jnp.zeros_like(value)), axis)  72.9 us
    scatter x1, local copies, waits for them, and re-layouts, local(): buffer = jnp.zeros((devices_all * SLOT, piece_rows, piece_cols), jnp.floa...  23.5 us
    dot_general x1, matrix products, local(): lax.dot_general(cross_rows, ainv_anc, (((1,), (1,)), ((), ())), preferred...  20.3 us
    all_to_all x1, starting transfers between devices, joined_exchange(): parts = lax.all_to_all(parts, axis, split_axis=0, concat_axis=0, tiled=True)  9.85 us
  transfers between devices with their start and end apart: 5, of which 4 were waited for; matrix products, arithmetic and copies ran while one was open for 13% of the time, Pallas kernels for 0%

commit v1 on v0

--- a/solution.py
+++ b/solution.py
@@ -2,6 +2,7 @@
 import jax.numpy as jnp
 from jax import lax
 from jax.sharding import PartitionSpec as P
+from jax.lax import all_to_all, axis_size
 
 W = 768
 AB = 128
@@ -59,7 +60,12 @@
         jnp.broadcast_to(keep_blocks[:, :, None], (1, block_count, AB)).reshape(1, local_rows) > 0
     )
     masked = jnp.where(keep_rows, l_panel, jnp.zeros_like(l_panel))
-    gathered = lax.all_gather(masked, "col", axis=0, tiled=True)
+
+    def _handle_series(mat, chip_axis):
+        value_now = jnp.concatenate([mat for _ in range(axis_size(chip_axis))], axis=0)
+        return all_to_all(value_now, chip_axis, 0, 0, tiled=True)
+
+    gathered = _handle_series(masked, "col")
     offset = col_index % group_ratio * cross_width
     own_cross = lax.dynamic_slice_in_dim(gathered, offset, cross_width, 1)
     cross_rows = broadcast(own_cross, "row", col_index // group_ratio)

time: 333 us -> 416 us (1.25)
  waiting for transfers between devices: 228 us -> 290 us
  other arithmetic: 19.5 us -> 28 us
  starting transfers between devices: 16.4 us -> 24.1 us
    all_to_all x0 -> x1, waiting for transfers between devices: none -> 139 us  [_handle_series(): return all_to_all(value_now, chip_axis, 0, 0, tiled=True)]
    all_gather x1 -> x0, waiting for transfers between devices: 79.1 us -> none  [local(): gathered = lax.all_gather(masked, 'col', axis=0, tiled=True)]
    unnamed x0 -> x15, other arithmetic: none -> 10.2 us
    all_to_all x0 -> x1, starting transfers between devices: none -> 7.62 us  [_handle_series(): return all_to_all(value_now, chip_axis, 0, 0, tiled=True)]
  transfers between devices with their start and end apart: 5 -> 5, of which waited for: 4 -> 4; matrix products, arithmetic and copies ran while one was open for 13% -> 10% of each run, Pallas kernels for 0% -> 0%
where the time goes in v1:
time: 416 us; the launch traced here: 414 us
  waiting for transfers between devices  290 us (70%)
  local copies, waits for them, and re-layouts  33.1 us (8%)
  other arithmetic  28 us (7%)
  matrix products  24.3 us (6%)
  starting transfers between devices  24.1 us (6%)
  between operations  14.4 us (3%)
    all_to_all x1, waiting for transfers between devices, _handle_series(): return all_to_all(value_now, chip_axis, 0, 0, tiled=True)  139 us
    psum x1, waiting for transfers between devices, broadcast(): return lax.psum(jnp.where(mine, value, jnp.zeros_like(value)), axis)  74.9 us
    reduce_scatter x1, waiting for transfers between devices, local(): lax.psum_scatter(lax.dot_general(cross_rows, ainv_anc, (((1,), (1,)), (()...  74.4 us
    scatter x1, local copies, waits for them, and re-layouts, local(): buffer = jnp.zeros((devices_all * SLOT, piece_rows, piece_cols), jnp.floa...  23.5 us
    dot_general x1, matrix products, local(): lax.dot_general(cross_rows, ainv_anc, (((1,), (1,)), ((), ())), preferred...  20.3 us
    unnamed x15, other arithmetic  10.2 us
    all_to_all x1, starting transfers between devices, joined_exchange(): parts = lax.all_to_all(parts, axis, split_axis=0, concat_axis=0, tiled=True)  9.89 us
  transfers between devices with their start and end apart: 5, of which 4 were waited for; matrix products, arithmetic and copies ran while one was open for 10% of the time, Pallas kernels for 0%

profile of v1, /device:TPU:1, one launch (start us, length us, event | category | flops | bytes accessed | tf_op | source)
XLA Modules:
  0.0 414.1 jit_solution(12537980777536657501)
XLA Ops:
  8.1 1.2 constant_dynamic-update-slice_fusion.15
  9.3 1.2 constant_dynamic-update-slice_fusion.14
  10.5 1.2 constant_dynamic-update-slice_fusion.13
  11.7 1.2 constant_dynamic-update-slice_fusion.12
  12.8 1.2 constant_dynamic-update-slice_fusion.11
  14.0 1.2 constant_dynamic-update-slice_fusion.10
  15.2 1.2 constant_dynamic-update-slice_fusion.9
  16.4 1.2 constant_dynamic-update-slice_fusion.8
  18.6 3.6 copy-done.1
  22.2 7.6 %all-to-all-start = ((bf16[16,96,3072]{2,1,0:T(8,128)(2,1)}), bf16[16,96,3072]{2,1,0:T(8,128)(2,1)}, u32[]{:S(2)}, u32[]{:S(2)}) async-start(bf16[16,96,3072]{2,1,0:T(8,128)(2,1)} %bitcast.41), calls=%async_computation | async-start | bytes 18874368 | tf_op jit(solution)/shard_map/all_to_all | solution.py:66
  29.9 138.9 %all-to-all-done = bf16[16,96,3072]{2,1,0:T(8,128)(2,1)} async-done(((bf16[16,96,3072]{2,1,0:T(8,128)(2,1)}), bf16[16,96,3072]{2,1,0:T(8,128)(2,1)}, u32[]{:S(2)}, u32[]{:S(2)}) %all-to-all-start) | async-done | bytes 9437216 | tf_op jit(solution)/shard_map/all_to_all | solution.py:66
  168.8 5.3 %dynamic-slice_select_fusion = bf16[1536,1536]{1,0:T(8,128)(2,1)} fusion(bf16[1536,3072]{1,0:T(8,128)(2,1)} %bitcast.3, s32[]{:T(128)S(6)} %select_n.53, pred[]{:T(512)S(6)} %eq.27), kind=kLoop, calls=%fused_computation.4 | loop fusion | flops 2359296 | bytes 9437189 | tf_op jit(solution)/shard_map/jit(_where)/select_n | solution.py:14
  174.2 74.9 %all-reduce.3.cloned.1.call-done = bf16[1536,1536]{1,0:T(8,128)(2,1)} async-done(((bf16[1536,1536]{1,0:T(8,128)(2,1)}), bf16[1536,1536]{1,0:T(8,128)(2,1)}) %all-reduce.3.cloned.1.call-update) | async-done | bytes 4718608 | tf_op jit(solution)/shard_map/psum | solution.py:14
  249.1 20.3 %convolution_convert_fusion = bf16[1536,3072]{1,0:T(8,128)(2,1)} fusion(bf16[1536,1536]{1,0:T(8,128)(2,1)} %all-reduce.3.cloned.1.call-done, bf16[3072,1536]{1,0:T(8,128)(2,1)} %param.6), kind=kOutput, calls=%fused_computation.1 | convolution fusion | flops 14500233216 | bytes 23592960 | tf_op jit(solution)/shard_map/dot_general | solution.py:73
  270.6 3.5 broadcast_in_dim.39
  274.2 23.5 %scatter_fusion = f32[384,32,128]{2,1,0:T(8,128)} fusion(f32[384,32,128]{2,1,0:T(8,128)} %broadcast_in_dim.39, s32[192]{0:T(256)S(1)} %bitcast.49, f32[192,32,128]{2,1,0:T(8,128)S(1)} %copy-done.2), kind=kCustom, calls=%fused_computation | custom fusion | bytes 9437952 | tf_op jit(solution)/shard_map/scatter | solution.py:100
  297.6 5.3 %convert_element_type.54 = bf16[384,32,128]{2,1,0:T(8,128)(2,1)} convert(f32[384,32,128]{2,1,0:T(8,128)} %scatter_fusion) | non-fusion elementwise | flops 1572864 | bytes 9437184 | tf_op jit(solution)/shard_map/convert_element_type | solution.py:104
  302.9 9.9 %all-to-all-start.2 = ((bf16[128,1,1,3,32,128]{5,4,3,2,1,0:T(8,128)(2,1)}), bf16[128,1,1,3,32,128]{5,4,3,2,1,0:T(8,128)(2,1)S(1)}, u32[]{:S(2)}, u32[]{:S(2)}) async-start(bf16[128,1,1,3,32,128]{5,4,3,2,1,0:T(8,128)(2,1)} %bitcast.40), calls=%async_computation.3 | async-start | bytes 6291456 | tf_op jit(solution)/shard_map/all_to_all | solution.py:40
  312.9 74.4 %reduce-scatter.2.cloned.1.call-done = bf16[96,3072]{1,0:T(8,128)(2,1)} async-done(((bf16[1536,3072]{1,0:T(8,128)(2,1)}), bf16[96,3072]{1,0:T(8,128)(2,1)}) %reduce-scatter.2.cloned.1.call-update) | async-done | bytes 589840 | tf_op jit(solution)/shard_map/reduce_scatter | solution.py:72
  387.3 1.2 select_convert_fusion
  389.3 3.9 fusion.2
  394.2 6.5 %all-to-all-start.1 = ((bf16[8,96,96]{2,1,0:T(8,128)(2,1)}), bf16[8,96,96]{2,1,0:T(8,128)(2,1)S(1)}, u32[]{:S(2)}, u32[]{:S(2)}) async-start(bf16[8,96,96]{2,1,0:T(8,128)(2,1)} %bitcast.36), calls=%async_computation.2 | async-start | bytes 393216 | tf_op jit(solution)/shard_map/all_to_all | solution.py:24
  400.8 3.8 bitcast_convert_fusion
  404.6 2.1 all-to-all-done.1
  (41 shorter events, 5.5 us)
Async XLA Ops:
  7.2 10.4 %copy-start = (bf16[96,3072]{1,0:T(8,128)(2,1)S(1)}, bf16[96,3072]{1,0:T(8,128)(2,1)}, u32[]{:S(2)}) copy-start(bf16[96,3072]{1,0:T(8,128)(2,1)} %param.7) | copy-start | bytes 1769476
  18.6 3.7 copy-start.1
  22.2 146.6 %all-to-all-start = ((bf16[16,96,3072]{2,1,0:T(8,128)(2,1)}), bf16[16,96,3072]{2,1,0:T(8,128)(2,1)}, u32[]{:S(2)}, u32[]{:S(2)}) async-start(bf16[16,96,3072]{2,1,0:T(8,128)(2,1)} %bitcast.41), calls=%async_computation | async-start | bytes 18874368 | tf_op jit(solution)/shard_map/all_to_all | solution.py:66
  29.9 219.2 %all-reduce.3.cloned.1.call-start = ((), (), s32[]{:S(2)}) async-start(), calls=%async_computation.4 | async-start | bytes 9437184 | tf_op jit(solution)/shard_map/psum | solution.py:14
  174.2 213.1 %reduce-scatter.2.cloned.1.call-start = ((), (), s32[]{:S(2)}) async-start(), calls=%async_computation.5 | async-start | bytes 10027008 | tf_op jit(solution)/shard_map/reduce_scatter | solution.py:72
  269.4 0.7 copy-start.5
  269.4 4.7 %copy-start.2 = (f32[192,32,128]{2,1,0:T(8,128)S(1)}, f32[192,32,128]{2,1,0:T(8,128)}, u32[]{:S(2)}) copy-start(f32[192,32,128]{2,1,0:T(8,128)} %param.10) | copy-start | bytes 9437188
  302.9 91.3 %all-to-all-start.2 = ((bf16[128,1,1,3,32,128]{5,4,3,2,1,0:T(8,128)(2,1)}), bf16[128,1,1,3,32,128]{5,4,3,2,1,0:T(8,128)(2,1)S(1)}, u32[]{:S(2)}, u32[]{:S(2)}) async-start(bf16[128,1,1,3,32,128]{5,4,3,2,1,0:T(8,128)(2,1)} %bitcast.40), calls=%async_computation.3 | async-start | bytes 6291456 | tf_op jit(solution)/shard_map/all_to_all | solution.py:40
  312.8 93.8 %copy-start.4 = (f32[96,96]{1,0:T(8,128)S(1)}, f32[96,96]{1,0:T(8,128)}, u32[]{:S(2)}) copy-start(f32[96,96]{1,0:T(8,128)} %param.8) | copy-start | bytes 110596
  388.5 0.8 copy-start.3
  394.2 12.4 %all-to-all-start.1 = ((bf16[8,96,96]{2,1,0:T(8,128)(2,1)}), bf16[8,96,96]{2,1,0:T(8,128)(2,1)S(1)}, u32[]{:S(2)}, u32[]{:S(2)}) async-start(bf16[8,96,96]{2,1,0:T(8,128)(2,1)} %bitcast.36), calls=%async_computation.2 | async-start | bytes 393216 | tf_op jit(solution)/shard_map/all_to_all | solution.py:24
Sparse Core Ops, SparseCore 0:
  174.3 74.7 all-reduce.2
  269.6 117.6 reduce-scatter.1
